TPU v7x, 16 devices: a whole 2x2x2 slice. The times are simulated.
16 devices in a mesh: dp: 1, ep: 16 (over x, y, z, core).
Axes of the slice: x: 2, y: 2, z: 2, core: 2. Of those that a mesh axis runs over, the one named last changes fastest.
Arguments:
- x: bfloat16 [1, 16, 256, 3584], P('dp', 'ep')
- expert: int32 [1, 16, 256, 8], P('dp', 'ep')
- slot: int32 [1, 16, 256, 8], P('dp', 'ep')
- gate: float32 [1, 16, 256, 8], P('dp', 'ep')
- w_gate: bfloat16 [48, 3584, 2048], P('ep')
- w_up: bfloat16 [48, 3584, 2048], P('ep')
- w_down: bfloat16 [48, 2048, 3584], P('ep')
- s_gate: bfloat16 [3584, 2048], replicated
- s_up: bfloat16 [3584, 2048], replicated
- s_down: bfloat16 [2048, 3584], replicated
Outputs:
- y: bfloat16 [1, 16, 256, 3584], P('dp', 'ep')
All inputs are finite; a program needn't handle non-finite values.
Results may differ from a plain program's by a relative error of at most 0.009.
Values are sent between devices in bfloat16 or wider.
A program may use at most 2 GiB of HBM per device.

v0:
```python
import jax
import jax.numpy as jnp
from jax import lax
from jax.sharding import NamedSharding, PartitionSpec as P


def einsum(form, a, b):
    return jnp.einsum(form, a.astype(jnp.float32), b.astype(jnp.float32))


def for_all(x, s_gate, s_up, s_down):
    h = jax.nn.silu(einsum("...d,df->...f", x, s_gate)) * einsum("...d,df->...f", x, s_up)
    return einsum("...f,fd->...d", h.astype(jnp.bfloat16), s_down)


def solution(mesh):
    def placed(v, *spec):
        return lax.with_sharding_constraint(v, NamedSharding(mesh, P(*spec)))

    def step(x, expert, slot, gate, w_gate, w_up, w_down, s_gate, s_up, s_down):
        experts, (tokens, top) = w_gate.shape[0], expert.shape[2:]
        slots = 5 * tokens * top // (4 * experts)
        to_expert = jax.nn.one_hot(expert, experts, dtype=jnp.bfloat16)
        to_slot = jax.nn.one_hot(slot, slots, dtype=jnp.bfloat16)
        weighted = to_expert * gate[..., None].astype(jnp.bfloat16)
        dispatch = einsum("abtke,abtkc->abtec", to_expert, to_slot).astype(jnp.bfloat16)
        combine = einsum("abtke,abtkc->abtec", weighted, to_slot).astype(jnp.bfloat16)
        z = einsum("abtec,abtd->aebcd", dispatch, x).astype(jnp.bfloat16)
        z = placed(z, "dp", None, "ep", None, None)
        z = placed(z, "dp", "ep", None, None, None)
        h = jax.nn.silu(einsum("aebcd,edf->aebcf", z, w_gate))
        h = (h * einsum("aebcd,edf->aebcf", z, w_up)).astype(jnp.bfloat16)
        out = einsum("aebcf,efd->aebcd", h, w_down).astype(jnp.bfloat16)
        out = placed(out, "dp", "ep", None, None, None)
        out = placed(out, "dp", None, "ep", None, None)
        y = einsum("abtec,aebcd->abtd", combine, out)
        return (y + for_all(x, s_gate, s_up, s_down)).astype(jnp.bfloat16)

    return step
```

profile of v0, /device:TPU:0, one launch (start us, length us, event | category | flops | bytes accessed | tf_op | source)
XLA Modules:
  0.0 738.9 jit_solution(7905739199279460450)
XLA Ops:
  0.0 0.0 copy-start
  0.0 1.0 copy.11
  1.0 0.0 copy-start.1
  1.0 0.8 copy.9
  1.8 0.0 copy-start.3
  1.8 3.2 convolution_convert_fusion.1
  5.0 0.0 copy-done
  5.0 10.3 %convolution_convert_fusion = bf16[48,53,3584]{2,1,0:T(8,128)(2,1)} fusion(bf16[256,48,53]{2,1,0:T(8,128)(2,1)S(1)} %convolution_convert_fusion.1, bf16[1,1,256,3584]{3,2,1,0:T(8,128)(2,1)S(1)} %copy-done), kind=kOutput, calls=%fused_computation.18 | convolution fusion | flops 4677378048 | bytes 21372928 | tf_op jit(solution)/abtec,abtd->aebcd/dot_general | solution.py:8
  15.4 0.0 copy-done.1
  15.4 0.0 copy-done.3
  15.4 218.4 %all-to-all.4 = bf16[1,16,3,1,53,3584]{5,4,2,3,0,1:T(8,128)(2,1)} all-to-all(bf16[1,16,3,1,53,3584]{5,4,2,3,0,1:T(8,128)(2,1)} %bitcast.143), channel_id=1, replica_groups=mesh['dp'=1,'ep'=16] {'ep'}, dimensions={1} | all-to-all | bytes 36470784 | tf_op jit(solution)/sharding_constraint;jit(solution)/sharding_constraint | solution.py:18
  233.8 47.7 %fusion.2 = f32[3,16,53,2048]{3,2,1,0:T(8,128)} fusion(bf16[3,3584,2048]{2,1,0:T(8,128)(2,1)} %param.5, bf16[1,16,3,1,53,3584]{5,4,2,3,0,1:T(8,128)(2,1)} %all-to-all.4), kind=kOutput, calls=%fused_computation.2 | convolution fusion | flops 37346082816 | bytes 83116032 | tf_op jit(solution)/aebcd,edf->aebcf/dot_general | solution.py:8
  281.5 47.7 %fusion.4 = f32[3,16,53,2048]{3,2,1,0:T(8,128)} fusion(bf16[3,3584,2048]{2,1,0:T(8,128)(2,1)} %param.4, bf16[1,16,3,1,53,3584]{5,4,2,3,0,1:T(8,128)(2,1)} %all-to-all.4), kind=kOutput, calls=%fused_computation.4 | convolution fusion | flops 37346082816 | bytes 83116032 | tf_op jit(solution)/aebcd,edf->aebcf/dot_general | solution.py:8
  329.2 56.2 %convert_bitcast_fusion = bf16[1,3,16,1,53,3584]{5,4,2,1,3,0:T(8,128)(2,1)} fusion(bf16[3,2048,3584]{2,1,0:T(8,128)(2,1)} %param.6, f32[3,16,53,2048]{3,2,1,0:T(8,128)} %fusion.2, f32[3,16,53,2048]{3,2,1,0:T(8,128)} %fusion.4), kind=kOutput, calls=%fused_computation.15 | convolution fusion | flops 37386461184 | bytes 103956480 | tf_op jit(solution)/aebcf,efd->aebcd/dot_general | solution.py:8
  385.4 15.6 %copy.15 = bf16[1,3,16,1,53,3584]{5,4,1,3,0,2:T(8,128)(2,1)} copy(bf16[1,3,16,1,53,3584]{5,4,2,1,3,0:T(8,128)(2,1)} %convert_bitcast_fusion) | data formatting | bytes 36470784 | tf_op jit(solution)/sharding_constraint;jit(solution)/sharding_constraint | solution.py:18
  400.9 0.0 copy-start.5
  400.9 0.0 copy-start.2
  400.9 0.0 copy-start.4
  400.9 4.2 all-to-all-start.1
  405.1 0.0 copy-done.5
  405.1 0.1 copy.10
  405.2 0.0 copy-done.2
  405.2 0.0 copy-done.4
  405.3 4.3 convolution_convert_fusion.2
  409.6 8.8 %convolution_bitcast_fusion.2 = f32[1,256,2048]{2,1,0:T(8,128)} fusion(bf16[3584,2048]{1,0:T(8,128)(2,1)} %param.7, bf16[1,1,256,3584]{3,2,1,0:T(8,128)(2,1)S(1)} %copy-done), kind=kOutput, calls=%fused_computation.28 | convolution fusion | flops 3758096384 | bytes 18612224 | tf_op jit(solution)/...d,df->...f/dot_general | solution.py:8
  418.4 19.8 %fusion.36 = f32[256,3584]{1,0:T(8,128)} fusion(bf16[2048,3584]{1,0:T(8,128)(2,1)} %param.9, bf16[3584,2048]{1,0:T(8,128)(2,1)} %param.8, f32[1,256,2048]{2,1,0:T(8,128)} %convolution_bitcast_fusion.2, bf16[1,1,256,3584]{3,2,1,0:T(8,128)(2,1)S(1)} %copy-done), kind=kOutput, calls=%fused_computation.41 | convolution fusion | flops 7519338496 | bytes 36962304 | tf_op jit(solution)/...f,fd->...d/dot_general | solution.py:8
  438.1 287.2 %all-to-all-done.1 = bf16[1,3,16,1,53,3584]{5,4,1,3,0,2:T(8,128)(2,1)} async-done(((bf16[1,3,16,1,53,3584]{5,4,1,3,0,2:T(8,128)(2,1)}), bf16[1,3,16,1,53,3584]{5,4,1,3,0,2:T(8,128)(2,1)}, u32[]{:S(2)}, u32[]{:S(2)}) %all-to-all-start.1) | async-done | bytes 18235424 | tf_op jit(solution)/sharding_constraint;jit(solution)/sharding_constraint | solution.py:18
  725.3 13.6 %fusion.20 = bf16[1,1,256,3584]{3,2,1,0:T(8,128)(2,1)} fusion(f32[256,3584]{1,0:T(8,128)} %fusion.36, bf16[48,53,3584]{2,1,0:T(8,128)(2,1)} %bitcast.37, bf16[256,48,53]{2,1,0:T(8,128)(2,1)} %convolution_convert_fusion.2), kind=kOutput, calls=%fused_computation.23 | convolution fusion | flops 4670095360 | bytes 25042944 | tf_op jit(solution)/abtec,aebcd->abtd/dot_general | solution.py:8
  (1 shorter events, 0.0 us)
Async XLA Ops:
  0.0 5.0 copy-start
  1.0 14.4 %copy-start.1 = (s32[256,8]{1,0:T(8,128)}, s32[256,8]{1,0:T(8,128)S(1)}, u32[]{:S(2)}) copy-start(s32[256,8]{1,0:T(8,128)S(1)} %copy.11) | copy-start | bytes 24580
  1.8 13.5 %copy-start.3 = (s32[256,8]{1,0:T(8,128)}, s32[256,8]{1,0:T(8,128)S(1)}, u32[]{:S(2)}) copy-start(s32[256,8]{1,0:T(8,128)S(1)} %copy.9) | copy-start | bytes 24580
  400.9 4.2 copy-start.5
  400.9 4.3 copy-start.2
  400.9 4.3 copy-start.4
  400.9 324.4 %all-to-all-start.1 = ((bf16[1,3,16,1,53,3584]{5,4,1,3,0,2:T(8,128)(2,1)}), bf16[1,3,16,1,53,3584]{5,4,1,3,0,2:T(8,128)(2,1)}, u32[]{:S(2)}, u32[]{:S(2)}) async-start(bf16[1,3,16,1,53,3584]{5,4,1,3,0,2:T(8,128)(2,1)} %copy.15), calls=%async_computation.1 | async-start | bytes 38535168 | tf_op jit(solution)/sharding_constraint;jit(solution)/sharding_constraint | solution.py:18
where the time goes:
time: 739 us
  waiting for transfers between devices  287 us (39%)
  blocking collectives  218 us (29%)
  matrix products  212 us (29%)
  local copies, waits for them, and re-layouts  17.5 us (2%)
    another operation x1, waiting for transfers between devices, placed(): return lax.with_sharding_constraint(v, NamedSharding(mesh, P(*spec)))  287 us
    another operation x1, blocking collectives, placed(): return lax.with_sharding_constraint(v, NamedSharding(mesh, P(*spec)))  218 us
    dot_general x9, matrix products, einsum(): return jnp.einsum(form, a.astype(jnp.float32), b.astype(jnp.float32))  212 us
    another operation x1, local copies, waits for them, and re-layouts, placed(): return lax.with_sharding_constraint(v, NamedSharding(mesh, P(*spec)))  15.6 us
  transfers between devices with their start and end apart: 1, of which 1 were waited for; matrix products, arithmetic and copies ran while one was open for 4% of the time, Pallas kernels for 0%

commit v1 on v0

v1 whole, which is shorter than its diff:
```python
import functools

import jax
import jax.numpy as jnp
from jax import lax
from jax.experimental import pallas as pl
from jax.experimental.pallas import tpu as pltpu
from jax.sharding import PartitionSpec as P

F32, BF16 = jnp.float32, jnp.bfloat16
CW = 512
PAD = 56
PARTS = ((0, 96, (8, 4, 2)), (96, 80, (4, 2, 8)), (176, 80, (2, 8, 4)))
VMEM_LIMIT = 67043328


def _dot(a, b):
    return lax.dot_general(a, b, (((1,), (0,)), ((), ())), preferred_element_type=F32)


def _place(axis):
    me = lax.axis_index(axis)
    bits = {8: me // 8, 4: (me // 4) % 2, 2: (me // 2) % 2, 1: me % 2}

    def flip(mask):
        d = me
        for b, v in bits.items():
            if mask & b:
                d = d + b * (1 - 2 * v)
        return d

    return me, bits, flip


def _greet(axis, others):
    barrier = pltpu.get_barrier_semaphore()
    for d in others:
        pl.semaphore_signal(barrier, inc=1, device_id={axis: d}, device_id_type=pl.DeviceIdType.MESH)
    pl.semaphore_wait(barrier, len(others))


def _wait(ref, sem):
    pltpu.make_async_copy(ref, ref, sem).wait()


def _up_kernel(
    axis, chunks, experts,
    x, meta, wg, wu, sg, su,
    xg, metag, h, hs,
    xv, xbuf, z, acc, wbuf, onehot, mv, stage,
    send_sem, phase_sem, pair_sem, meta_send, meta_recv, wsem, xsem, lsem, hsem,
):
    me, bits, flip = _place(axis)
    tokens, ff = x.shape[0], wg.shape[2]
    tiles = ff // 512

    def cols(n):
        return pl.ds(pl.multiple_of(n * CW, CW), CW)

    def remote(src, dst, send, recv, mask):
        pltpu.make_async_remote_copy(
            src_ref=src, dst_ref=dst, send_sem=send, recv_sem=recv,
            device_id={axis: flip(mask)}, device_id_type=pl.DeviceIdType.MESH,
        ).start()

    def send(block, n, i, to, phase):
        lo, size, _ = PARTS[i]
        d = flip(block)
        there = xg.at[d, pl.ds(lo, size), cols(n)]
        here = x.at[pl.ds(lo, size), cols(n)] if block == 0 else there
        recv = pair_sem.at[n] if to == 1 else phase_sem.at[n, i, phase]
        remote(here, there, send_sem, recv, to)

    def t0(n):
        for phase in range(3):
            for i, (_, _, dims) in enumerate(PARTS):
                send(0, n, i, dims[phase], phase)
        remote(x.at[:, cols(n)], xg.at[me, :, cols(n)], send_sem, pair_sem.at[n], 1)

    def arrived(n, i, phase, blocks):
        lo, size, _ = PARTS[i]
        _wait(xg.at[pl.ds(0, blocks), pl.ds(lo, size), cols(n)], phase_sem.at[n, i, phase])

    def t1(n):
        for i, (_, _, (a, b, c)) in enumerate(PARTS):
            arrived(n, i, 0, 1)
            send(a, n, i, b, 1)
            send(a, n, i, c, 2)
            send(a, n, i, 1, 0)

    def t2(n):
        for i, (_, _, (a, b, c)) in enumerate(PARTS):
            arrived(n, i, 1, 2)
            for block in (b, a + b):
                send(block, n, i, c, 2)
                send(block, n, i, 1, 0)

    def t3(n):
        for i, (_, _, (a, b, c)) in enumerate(PARTS):
            arrived(n, i, 2, 4)
            for block in (c, a + c, b + c, a + b + c):
                send(block, n, i, 1, 0)

    def t4(n):
        _wait(xg.at[pl.ds(0, 8), :, cols(n)], pair_sem.at[n])
        for block in range(16):
            d = flip(block)
            src = x.at[:, cols(n)] if block == 0 else xg.at[d, :, cols(n)]
            pltpu.make_async_copy(src, xbuf.at[d], xsem).start()

    def weights(n, e, slot):
        for half, w in enumerate((wg, wu)):
            pltpu.make_async_copy(w.at[e, cols(n), :], wbuf.at[slot, half], wsem.at[slot, half]).start()

    def shared_weights(k, slot):
        for half, w in enumerate((sg, su)):
            pltpu.make_async_copy(w.at[cols(k), :], wbuf.at[slot, half], wsem.at[slot, half]).start()

    def have(slot, half):
        _wait(wbuf.at[slot, half], wsem.at[slot, half])

    own = pltpu.make_async_copy(x, xv, lsem)
    own.start()
    shared_weights(0, 0)
    _greet(axis, [flip(m) for m in range(1, 16)])
    t0(0)
    for m in range(1, 16):
        d = flip(m)
        remote(meta.at[d], metag.at[me], meta_send, meta_recv, m)
    t0(1)
    acc[0, pl.ds(0, tokens), :] = jnp.zeros((tokens, 2 * ff), F32)
    own.wait()

    for k in range(chunks):
        slot = k % 2
        if k + 1 < chunks:
            shared_weights(k + 1, 1 - slot)
        else:
            weights(0, 0, 1 - slot)
        for half in range(2):
            have(slot, half)

            def tile(j, _):
                at = pl.ds(pl.multiple_of(half * ff + j * 512, 512), 512)
                w = wbuf[slot, half, :, pl.ds(pl.multiple_of(j * 512, 512), 512)]
                acc[0, pl.ds(0, tokens), at] += _dot(xv[:, k * CW:(k + 1) * CW], w)
                return 0

            lax.fori_loop(0, tiles, tile, 0)
        if k == 1:
            _wait(metag.at[pl.ds(0, 15)], meta_recv)
            for m in range(16):
                d = flip(m)
                pltpu.make_async_copy(meta.at[d] if m == 0 else metag.at[d], mv.at[d], lsem).start()
            t1(0)
        if k == 4:
            t2(0)

    def shared_h(j, _):
        g = acc[0, pl.ds(0, tokens), pl.ds(pl.multiple_of(j * 512, 512), 512)]
        u = acc[0, pl.ds(0, tokens), pl.ds(pl.multiple_of(ff + j * 512, 512), 512)]
        v = (g * jax.nn.sigmoid(g) * u).astype(BF16)
        xv[:, pl.ds(pl.multiple_of(j * 512, 512), 512)] = v
        return 0

    lax.fori_loop(0, tiles, shared_h, 0)
    hs_out = pltpu.make_async_copy(xv.at[:, pl.ds(0, ff)], hs, hsem.at[2])
    hs_out.start()

    _wait(mv, lsem)
    pltpu.make_async_copy(mv.at[me], metag.at[me], lsem).start()
    row = lax.broadcasted_iota(jnp.int32, (PAD, tokens), 0).astype(F32)

    def build(s, _):
        pos = mv[s].astype(F32)
        for e in range(experts):
            hit = jnp.where(pos[e:e + 1, :] == row, 1.0, 0.0)
            onehot[s, e] = hit.astype(BF16)
        return 0

    lax.fori_loop(0, 16, build, 0)
    t3(0)
    t4(0)

    def chunk(n, first, last):
        _wait(xbuf, xsem)

        def pair(p, _):
            got = []
            for i in range(2):
                s = 2 * p + i
                m = jnp.concatenate([onehot[s, e] for e in range(experts)], 0)
                got.append(_dot(m, xbuf[s]))
            for e in range(experts):
                both = jnp.concatenate([v[PAD * e:PAD * (e + 1)] for v in got], 0)
                z[e, pl.ds(pl.multiple_of(p * 2 * PAD, 16), 2 * PAD), :] = both.astype(BF16)
            return 0

        lax.fori_loop(0, 8, pair, 0)

        for e in range(experts):
            slot = (chunks + experts * n + e) % 2
            if e + 1 < experts:
                weights(n, e + 1, 1 - slot)
            elif not last:
                weights(n + 1, 0, 1 - slot)
            if last:
                have(slot, 0)
                have(slot, 1)

                def finish(j, _):
                    at = pl.ds(pl.multiple_of(j * 512, 512), 512)
                    at_u = pl.ds(pl.multiple_of(ff + j * 512, 512), 512)
                    side = j % 2

                    @pl.when(e * tiles + j >= 2)
                    def _():
                        _wait(stage.at[side], hsem.at[side])

                    def rows(i, _):
                        r = pl.ds(pl.multiple_of(i * 224, 224), 224)
                        g = acc[e, r, at] + _dot(z[e, r, :], wbuf[slot, 0, :, at])
                        u = acc[e, r, at_u] + _dot(z[e, r, :], wbuf[slot, 1, :, at])
                        stage[side, r, :] = (g * jax.nn.sigmoid(g) * u).astype(BF16)
                        return 0

                    lax.fori_loop(0, 16 * PAD // 224, rows, 0)
                    pltpu.make_async_copy(stage.at[side], h.at[e, :, at], hsem.at[side]).start()
                    return 0

                lax.fori_loop(0, tiles, finish, 0)
            else:
                for half in range(2):
                    have(slot, half)

                    def tile(j, _):
                        at = pl.ds(pl.multiple_of(half * ff + j * 512, 512), 512)
                        w = wbuf[slot, half, :, pl.ds(pl.multiple_of(j * 512, 512), 512)]
                        if first:
                            acc[e, :, at] = _dot(z[e], w)
                        else:
                            acc[e, :, at] += _dot(z[e], w)
                        return 0

                    lax.fori_loop(0, tiles, tile, 0)
                    point = 2 * e + half
                    if point == 0:
                        t1(n + 1)
                    if point == 2:
                        t2(n + 1)
                    if point == 3:
                        @pl.when(n + 2 < chunks)
                        def _():
                            t0(n + 2)
                    if point == 4:
                        t3(n + 1)
        if not last:
            t4(n + 1)

    chunk(0, True, False)

    def middle(n, _):
        chunk(n, False, False)
        return 0

    lax.fori_loop(1, chunks - 1, middle, 0)
    chunk(chunks - 1, False, True)
    for side in range(2):
        _wait(stage.at[side], hsem.at[side])
    hs_out.wait()
    _wait(mv.at[0], lsem)
    _wait(metag.at[pl.ds(0, 15)], meta_send)
    _wait(xg.at[pl.ds(0, 15)], send_sem)


def _down_kernel(
    axis, chunks, experts,
    h, hs, metag, wd, sd,
    y,
    hv, hsv, out32, wbuf, weight_t, mv, own, give, take, s1, s2, s3, r1, r2, r3, ost,
    hsem, lsem, wsem, give_sem, take_sem, credit, ss1, ss2, ss3, rs1, rs2, rs3, osem,
):
    me, bits, flip = _place(axis)
    tokens = hs.shape[0]

    def cols(n):
        return pl.ds(pl.multiple_of(n * CW, CW), CW)

    def remote(src, dst, send, recv, mask):
        pltpu.make_async_remote_copy(
            src_ref=src, dst_ref=dst, send_sem=send, recv_sem=recv,
            device_id={axis: flip(mask)}, device_id_type=pl.DeviceIdType.MESH,
        ).start()

    def weights(n, e, slot):
        src = wd.at[e, :, cols(n)] if e < experts else sd.at[:, cols(n)]
        pltpu.make_async_copy(src, wbuf.at[slot], wsem.at[slot]).start()

    for e in range(experts):
        pltpu.make_async_copy(h.at[e], hv.at[e], hsem.at[e]).start()
    weights(0, 0, 0)
    pltpu.make_async_copy(hs, hsv, hsem.at[experts]).start()
    copy = pltpu.make_async_copy(metag, mv, lsem)
    copy.start()
    _greet(axis, [flip(m) for m in (8, 4, 2, 1)])
    copy.wait()

    row = lax.broadcasted_iota(jnp.int32, (PAD, tokens), 0).astype(F32)
    rest = jnp.zeros((256 - experts * PAD, tokens), F32)

    def build(s, _):
        v = mv[s].astype(F32)
        hits = [jnp.where(v[e:e + 1, :] == row, v[experts + e:experts + e + 1, :], 0.0) for e in range(experts)]
        weight_t[s] = jnp.transpose(jnp.concatenate([*hits, rest], 0)).astype(BF16)
        return 0

    lax.fori_loop(0, 16, build, 0)

    def part(i):
        lo, size, dims = PARTS[i]
        return pl.ds(lo, size), dims

    def f32(ref, *at):
        return ref[at].astype(F32)

    def sum_at(n, block, r):
        p = n % 2
        return own[p, block // 2, r, :] + f32(take, p, block // 2, r, slice(None))

    def stage1(n):
        p = n % 2
        _wait(take.at[p], take_sem.at[p])

        @pl.when(n >= 2)
        def _():
            _wait(s1.at[p], ss1.at[p])

        for i in range(3):
            r, (a, b, c) = part(i)
            for k, q in enumerate((b + c, b, c, 0)):
                s1[p, k, r, :] = sum_at(n, q + a, r).astype(BF16)
                remote(s1.at[p, k, r], r1.at[n, k, r], ss1.at[p], rs1.at[n, i, k], a)

    def stage2(n):
        p = n % 2

        @pl.when(n >= 2)
        def _():
            _wait(s2.at[p], ss2.at[p])

        for i in range(3):
            r, (a, b, c) = part(i)
            for k, q in enumerate((b + c, b)):
                _wait(r1.at[n, k, r], rs1.at[n, i, k])
                v = sum_at(n, q, r) + f32(r1, n, k, r, slice(None))
                s2[p, k, r, :] = v.astype(BF16)
                remote(s2.at[p, k, r], r2.at[n, k, r], ss2.at[p], rs2.at[n, i, k], b)

    def stage3(n):
        p = n % 2

        @pl.when(n >= 2)
        def _():
            _wait(s3.at[p], ss3.at[p])

        for i in range(3):
            r, (a, b, c) = part(i)
            _wait(r1.at[n, 2, r], rs1.at[n, i, 2])
            _wait(r2.at[n, 0, r], rs2.at[n, i, 0])
            v = sum_at(n, c, r) + f32(r1, n, 2, r, slice(None)) + f32(r2, n, 0, r, slice(None))
            s3[p, r, :] = v.astype(BF16)
            remote(s3.at[p, r], r3.at[n, r], ss3.at[p], rs3.at[n, i], c)

    def stage4(n):
        p = n % 2

        @pl.when(n >= 2)
        def _():
            _wait(ost.at[p], osem.at[p])

        for i in range(3):
            r, (a, b, c) = part(i)
            _wait(r1.at[n, 3, r], rs1.at[n, i, 3])
            _wait(r2.at[n, 1, r], rs2.at[n, i, 1])
            _wait(r3.at[n, r], rs3.at[n, i])
            v = sum_at(n, 0, r) + f32(r1, n, 3, r, slice(None)) + f32(r2, n, 1, r, slice(None))
            ost[p, r, :] = (v + f32(r3, n, r, slice(None))).astype(BF16)
        pltpu.make_async_copy(ost.at[p], y.at[:, cols(n)], osem.at[p]).start()
        pl.semaphore_signal(credit, inc=1, device_id={axis: flip(1)}, device_id_type=pl.DeviceIdType.MESH)

    for e in range(experts + 1):
        _wait(hv.at[e] if e < experts else hsv, hsem.at[e])

    def combine(r, core):
        s = 8 * ((bits[8] + r // 4) % 2) + 4 * ((bits[4] + (r // 2) % 2) % 2) + 2 * ((bits[2] + r % 2) % 2) + core
        at = pl.ds(pl.multiple_of(s * PAD, 8), PAD)
        rest = jnp.zeros((256 - experts * PAD, CW), F32)
        v = jnp.concatenate([*(out32[e, at, :] for e in range(experts)), rest], 0).astype(BF16)
        return _dot(weight_t[s], v)

    def chunk(n, _):
        p = n % 2
        for e in range(experts):
            slot = e % 2
            weights(n, e + 1, 1 - slot)
            _wait(wbuf.at[slot], wsem.at[slot])
            out32[e] = _dot(hv[e], wbuf[slot])
            if e == 0:
                @pl.when(n >= 1)
                def _():
                    stage1(n - 1)
            if e == 1:
                @pl.when(n >= 2)
                def _():
                    stage3(n - 2)
            if e == 2:
                @pl.when(n >= 2)
                def _():
                    stage4(n - 2)

        @pl.when(n + 1 < chunks)
        def _():
            weights(n + 1, 0, 0)

        @pl.when(n >= 2)
        def _():
            _wait(give.at[p], give_sem.at[p])
            pl.semaphore_wait(credit, 1)

        def others(r, _):
            give[p, r] = combine(r, 1 - bits[1]).astype(BF16)
            remote(give.at[p, r], take.at[p, r], give_sem.at[p], take_sem.at[p], 1)
            return 0

        lax.fori_loop(0, 8, others, 0)

        @pl.when(n >= 1)
        def _():
            stage2(n - 1)

        def mine(r, _):
            own[p, r] = combine(r, bits[1])
            return 0

        lax.fori_loop(1, 8, mine, 0)
        _wait(wbuf.at[1], wsem.at[1])
        own[p, 0] = combine(0, bits[1]) + _dot(hsv[...], wbuf[1])
        return 0

    lax.fori_loop(0, chunks, chunk, 0)
    stage1(chunks - 1)
    stage3(chunks - 2)
    stage4(chunks - 2)
    stage2(chunks - 1)
    stage3(chunks - 1)
    stage4(chunks - 1)
    for p in range(2):
        _wait(give.at[p], give_sem.at[p])
        _wait(s1.at[p], ss1.at[p])
        _wait(s2.at[p], ss2.at[p])
        _wait(s3.at[p], ss3.at[p])
        _wait(ost.at[p], osem.at[p])
    pl.semaphore_wait(credit, 2)


def _table(expert, slot, gate, members, experts, slots):
    tokens, top = expert.shape
    hit = expert[None] == jnp.arange(members * experts, dtype=jnp.int32)[:, None, None]
    hit = hit & (slot < slots)[None]
    pos = jnp.sum(jnp.where(hit, slot[None] + 1, 0), axis=-1) - 1
    weight = jnp.sum(jnp.where(hit, gate.astype(BF16).astype(F32)[None], 0.0), axis=-1)
    pos = pos.astype(BF16).reshape(members, experts, tokens)
    weight = weight.astype(BF16).reshape(members, experts, tokens)
    rest = jnp.zeros((members, 16 - 2 * experts, tokens), BF16)
    return jnp.concatenate([pos, weight, rest], axis=1)


def solution(mesh):
    axis, members = "ep", mesh.shape["ep"]

    def local(x, expert, slot, gate, w_gate, w_up, w_down, s_gate, s_up, s_down):
        x, expert, slot, gate = x[0, 0], expert[0, 0], slot[0, 0], gate[0, 0]
        tokens, d = x.shape
        experts, _, ff = w_gate.shape
        slots = 5 * tokens * expert.shape[1] // (4 * experts * members)
        chunks, rows = d // CW, members * PAD
        meta = _table(expert, slot, gate, members, experts, slots)
        hbm, dma = pl.BlockSpec(memory_space=pl.ANY), pltpu.SemaphoreType.DMA
        _, metag, h, hs = pl.pallas_call(
            functools.partial(_up_kernel, axis, chunks, experts),
            name="gather_up",
            out_shape=(
                jax.ShapeDtypeStruct((members, tokens, d), BF16),
                jax.ShapeDtypeStruct(meta.shape, BF16),
                jax.ShapeDtypeStruct((experts, rows, ff), BF16),
                jax.ShapeDtypeStruct((tokens, ff), BF16),
            ),
            in_specs=[hbm] * 6,
            out_specs=(hbm,) * 4,
            scratch_shapes=[
                pltpu.VMEM((tokens, d), BF16),
                pltpu.VMEM((members, tokens, CW), BF16),
                pltpu.VMEM((experts, rows, CW), BF16),
                pltpu.VMEM((experts, rows, 2 * ff), F32),
                pltpu.VMEM((2, 2, CW, ff), BF16),
                pltpu.VMEM((members, experts, PAD, tokens), BF16),
                pltpu.VMEM(meta.shape, BF16),
                pltpu.VMEM((2, rows, 512), BF16),
                dma, dma((chunks, 3, 3)), dma((chunks,)), dma, dma, dma((2, 2)), dma, dma, dma((3,)),
            ],
            compiler_params=pltpu.CompilerParams(
                collective_id=0, has_side_effects=True, vmem_limit_bytes=VMEM_LIMIT
            ),
        )(x, meta, w_gate, w_up, s_gate, s_up)
        y = pl.pallas_call(
            functools.partial(_down_kernel, axis, chunks, experts),
            name="down_scatter",
            out_shape=jax.ShapeDtypeStruct((tokens, d), BF16),
            in_specs=[hbm] * 5,
            out_specs=hbm,
            scratch_shapes=[
                pltpu.VMEM((experts, rows, ff), BF16),
                pltpu.VMEM((tokens, ff), BF16),
                pltpu.VMEM((experts, rows, CW), F32),
                pltpu.VMEM((2, ff, CW), BF16),
                pltpu.VMEM((members, tokens, 256), BF16),
                pltpu.VMEM(meta.shape, BF16),
                pltpu.VMEM((2, 8, tokens, CW), F32),
                pltpu.VMEM((2, 8, tokens, CW), BF16),
                pltpu.VMEM((2, 8, tokens, CW), BF16),
                pltpu.VMEM((2, 4, tokens, CW), BF16),
                pltpu.VMEM((2, 2, tokens, CW), BF16),
                pltpu.VMEM((2, tokens, CW), BF16),
                pltpu.VMEM((chunks, 4, tokens, CW), BF16),
                pltpu.VMEM((chunks, 2, tokens, CW), BF16),
                pltpu.VMEM((chunks, tokens, CW), BF16),
                pltpu.VMEM((2, tokens, CW), BF16),
                dma((experts + 1,)), dma, dma((2,)), dma((2,)), dma((2,)), pltpu.SemaphoreType.REGULAR,
                dma((2,)), dma((2,)), dma((2,)),
                dma((chunks, 3, 4)), dma((chunks, 3, 2)), dma((chunks, 3)), dma((2,)),
            ],
            compiler_params=pltpu.CompilerParams(
                collective_id=1, has_side_effects=True, vmem_limit_bytes=VMEM_LIMIT
            ),
        )(h, hs, metag, w_down, s_down)
        return y[None, None]

    tok = P("dp", "ep", None, None)
    own = P("ep", None, None)
    return jax.shard_map(
        local,
        mesh=mesh,
        in_specs=(tok, tok, tok, tok, own, own, own, P(), P(), P()),
        out_specs=tok,
        check_vma=False,
    )
```

time: 739 us -> 342 us (0.46)
  Pallas kernels: 0 us -> 334 us
  waiting for transfers between devices: 287 us -> 0 us
  blocking collectives: 218 us -> 0 us
  matrix products: 212 us -> 0 us
  local copies, waits for them, and re-layouts: 17.5 us -> 2.97 us
    pallas_call x0 -> x2, Pallas kernels: none -> 334 us  [the longest x1 185 us: local(): pl.pallas_call(functools.partial(_up_kernel, axis, chunks, experts), name...]
    another operation x1 -> x0, waiting for transfers between devices: 287 us -> none  [placed(): return lax.with_sharding_constraint(v, NamedSharding(mesh, P(*spec)))]
    another operation x1 -> x0, blocking collectives: 218 us -> none  [placed(): return lax.with_sharding_constraint(v, NamedSharding(mesh, P(*spec)))]
    dot_general x9 -> x0, matrix products: 212 us -> none  [einsum(): return jnp.einsum(form, a.astype(jnp.float32), b.astype(jnp.float32))]
    another operation x1 -> x0, local copies, waits for them, and re-layouts: 15.6 us -> none  [placed(): return lax.with_sharding_constraint(v, NamedSharding(mesh, P(*spec)))]
  transfers between devices with their start and end apart: 1 -> 0, of which waited for: 1 -> 0; matrix products, arithmetic and copies ran while one was open for 4% -> 0% of each run, Pallas kernels for 0% -> 0%
where the time goes in v1:
time: 342 us
  Pallas kernels  334 us (98%)
  other arithmetic  4.57 us (1%)
    pallas_call x1, Pallas kernels, local(): pl.pallas_call(functools.partial(_up_kernel, axis, chunks, experts), name...  185 us
    pallas_call x1, Pallas kernels, local(): pl.pallas_call(functools.partial(_down_kernel, axis, chunks, experts), na...  150 us

profile of v1, /device:TPU:0, one launch (start us, length us, event | category | flops | bytes accessed | tf_op | source)
XLA Modules:
  0.0 341.9 jit_solution(648284064519526470)
XLA Ops:
  0.0 0.1 pad.2.clone
  0.1 0.7 compare_bitcast_fusion
  0.8 0.7 bitcast_convert_fusion
  1.5 0.7 add_bitcast_fusion
  2.2 0.9 select_reduce_fusion
  3.1 0.9 select_reduce_fusion.1
  4.0 0.7 maximum_maximum_fusion.meta
  4.7 184.6 %gather_up.1 = (bf16[16,256,3584]{2,1,0:T(8,128)(2,1)}, bf16[16,16,256]{2,1,0:T(8,128)(2,1)}, bf16[3,896,2048]{2,1,0:T(8,128)(2,1)}, bf16[256,2048]{1,0:T(8,128)(2,1)}) custom-call(bf16[256,3584]{1,0:T(8,128)(2,1)} %bitcast.11, bf16[16,16,256]{2,1,0:T(8,128)(2,1)} %maximum_maximum_fusion.meta, bf16[3,3584,2048]{2,1,0:T(8,128)(2,1)} %wg.1, ...), custom_call_target="tpu_custom_call" | custom-call | tf_op jit(solution)/shard_map/gather_up/pallas_call | solution.py:489
  189.4 149.7 %down_scatter.1 = bf16[256,3584]{1,0:T(8,128)(2,1)} custom-call(bf16[3,896,2048]{2,1,0:T(8,128)(2,1)} %get-tuple-element.8.h, bf16[256,2048]{1,0:T(8,128)(2,1)} %get-tuple-element.9.hs, bf16[16,16,256]{2,1,0:T(8,128)(2,1)} %get-tuple-element.10.metag, bf16[3,2048,3584]{2,1,0:T(8,128)(2,1)} %wd.1, bf16[2048,3584]{1,0:T(8,128)(2,1)} %sd.1), custom_call_target="tpu_custom_call" | custom-call | tf_op jit(solution)/shard_map/down_scatter/pallas_call | solution.py:515
  339.1 2.8 copy.20
  (4 shorter events, 0.1 us)

commit v2 on v1

v2 whole, which is shorter than its diff:
```python
import functools

import jax
import jax.numpy as jnp
from jax import lax
from jax.experimental import pallas as pl
from jax.experimental.pallas import tpu as pltpu
from jax.sharding import PartitionSpec as P

F32, BF16 = jnp.float32, jnp.bfloat16
CW = 512
CB = 512
WIN = 64
NONE = -1024.0
LAG = 3
PARTS = ((0, 96, (8, 4, 2)), (96, 80, (4, 2, 8)), (176, 80, (2, 8, 4)))
VMEM_LIMIT = 67043328


def _dot(a, b):
    return lax.dot_general(a, b, (((1,), (0,)), ((), ())), preferred_element_type=F32)


def _place(axis):
    me = lax.axis_index(axis)
    bits = {8: me // 8, 4: (me // 4) % 2, 2: (me // 2) % 2, 1: me % 2}

    def flip(mask):
        d = me
        for b, v in bits.items():
            if mask & b:
                d = d + b * (1 - 2 * v)
        return d

    return me, bits, flip


def _greet(axis, others):
    barrier = pltpu.get_barrier_semaphore()
    for d in others:
        pl.semaphore_signal(barrier, inc=1, device_id={axis: d}, device_id_type=pl.DeviceIdType.MESH)
    pl.semaphore_wait(barrier, len(others))


def _wait(ref, sem):
    pltpu.make_async_copy(ref, ref, sem).wait()


def _up_kernel(
    axis, chunks, experts, slots,
    x, expert, slot, gate, wg, wu, sg, su,
    xg, metag, h, hs,
    xbuf, z, acc, wbuf, onehot, ev, sv, gv, mt, mv,
    send_sem, phase_sem, pair_sem, meta_send, meta_recv, wsem, xsem, lsem, rsem, hsem,
):
    me, bits, flip = _place(axis)
    tokens, ff = x.shape[0], wg.shape[2]
    rows = 16 * slots

    def cols(n):
        return pl.ds(pl.multiple_of(n * CW, CW), CW)

    def remote(src, dst, send, recv, mask):
        pltpu.make_async_remote_copy(
            src_ref=src, dst_ref=dst, send_sem=send, recv_sem=recv,
            device_id={axis: flip(mask)}, device_id_type=pl.DeviceIdType.MESH,
        ).start()

    def send(block, n, i, to, phase):
        lo, size, _ = PARTS[i]
        d = flip(block)
        there = xg.at[d, pl.ds(lo, size), cols(n)]
        here = x.at[pl.ds(lo, size), cols(n)] if block == 0 else there
        recv = pair_sem.at[n] if to == 1 else phase_sem.at[n, i, phase]
        remote(here, there, send_sem, recv, to)

    def t0(n, *phases):
        for phase in phases:
            for i, (_, _, dims) in enumerate(PARTS):
                send(0, n, i, dims[phase], phase)
        if 2 in phases:
            remote(x.at[:, cols(n)], xg.at[me, :, cols(n)], send_sem, pair_sem.at[n], 1)

    def arrived(n, i, phase, blocks):
        lo, size, _ = PARTS[i]
        _wait(xg.at[pl.ds(0, blocks), pl.ds(lo, size), cols(n)], phase_sem.at[n, i, phase])

    def t1(n):
        for i, (_, _, (a, b, c)) in enumerate(PARTS):
            arrived(n, i, 0, 1)
            send(a, n, i, b, 1)
            send(a, n, i, c, 2)
            send(a, n, i, 1, 0)

    def t2(n):
        for i, (_, _, (a, b, c)) in enumerate(PARTS):
            arrived(n, i, 1, 2)
            for block in (b, a + b):
                send(block, n, i, c, 2)
                send(block, n, i, 1, 0)

    def t3(n):
        for i, (_, _, (a, b, c)) in enumerate(PARTS):
            arrived(n, i, 2, 4)
            for block in (c, a + c, b + c, a + b + c):
                send(block, n, i, 1, 0)

    def block_rows(s):
        return pl.ds(pl.multiple_of(s * tokens, tokens), tokens)

    def t4(n):
        _wait(xg.at[pl.ds(0, 8), :, cols(n)], pair_sem.at[n])
        for block in range(16):
            d = flip(block)
            src = x.at[:, cols(n)] if block == 0 else xg.at[d, :, cols(n)]
            pltpu.make_async_copy(src, xbuf.at[block_rows(d)], xsem).start()

    def weights(n, e, side):
        for half, w in enumerate((wg, wu)):
            pltpu.make_async_copy(w.at[e, cols(n), :], wbuf.at[side, half], wsem.at[side, half]).start()

    def shared_weights(k, side):
        for half, w in enumerate((sg, su)):
            pltpu.make_async_copy(w.at[cols(k), :], wbuf.at[side, half], wsem.at[side, half]).start()

    def have(side, half):
        _wait(wbuf.at[side, half], wsem.at[side, half])

    for k in range(chunks):
        pltpu.make_async_copy(x.at[:, cols(k)], xbuf.at[block_rows(k)], lsem).start()
    routing = [pltpu.make_async_copy(a, b, rsem.at[i]) for i, (a, b) in enumerate(((expert, ev), (slot, sv), (gate, gv)))]
    for copy in routing:
        copy.start()
    shared_weights(0, 0)
    _greet(axis, [flip(m) for m in range(1, 16)])
    t0(0, 0, 1, 2)

    for copy in routing:
        copy.wait()

    et, st, gt = ev[...].astype(F32), sv[...].astype(F32), gv[...].astype(BF16).astype(F32)
    kept = st < slots

    def table(d, _):
        pos, weight = [], []
        for j in range(experts):
            hit = (et == (experts * d + j).astype(F32)) & kept
            pos.append(jnp.sum(jnp.where(hit, st - NONE, 0.0), axis=0, keepdims=True) + NONE)
            weight.append(jnp.sum(jnp.where(hit, gt, 0.0), axis=0, keepdims=True))
        rest = jnp.zeros((16 - 2 * experts, tokens), F32)
        mt[d] = jnp.concatenate([*pos, *weight, rest], 0).astype(BF16)
        return 0

    lax.fori_loop(0, 16, table, 0)
    for m in range(1, 16):
        remote(mt.at[flip(m)], mv.at[me], meta_send, meta_recv, m)
    mv[me] = mt[me]
    acc[0, pl.ds(0, tokens), :] = jnp.zeros((tokens, 2 * ff), F32)
    _wait(xbuf.at[pl.ds(0, chunks * tokens)], lsem)

    for k in range(chunks):
        side = k % 2
        if k + 1 < chunks:
            shared_weights(k + 1, 1 - side)
        else:
            weights(0, 0, 1 - side)
        for half in range(2):
            have(side, half)
            acc[0, pl.ds(0, tokens), pl.ds(half * ff, ff)] += _dot(xbuf[pl.ds(k * tokens, tokens), :], wbuf[side, half])
        if k == 1:
            t1(0)
        if k == 4:
            t2(0)
            t0(1, 0, 1, 2)

    def shared_h(j, _):
        g = acc[0, pl.ds(0, tokens), pl.ds(pl.multiple_of(j * 512, 512), 512)]
        u = acc[0, pl.ds(0, tokens), pl.ds(pl.multiple_of(ff + j * 512, 512), 512)]
        there = block_rows(chunks + j)
        xbuf[there, :] = (g * jax.nn.sigmoid(g) * u).astype(BF16)
        pltpu.make_async_copy(xbuf.at[there], hs.at[:, pl.ds(pl.multiple_of(j * 512, 512), 512)], lsem).start()
        return 0

    lax.fori_loop(0, ff // 512, shared_h, 0)

    _wait(mv.at[pl.ds(0, 15)], meta_recv)
    meta_out = pltpu.make_async_copy(mv, metag, rsem.at[0])
    meta_out.start()
    row = lax.broadcasted_iota(jnp.int32, (WIN, tokens), 0).astype(F32)

    def build(s, _):
        pos = mv[s].astype(F32) + ((s * slots) % 8).astype(F32)
        for e in range(experts):
            onehot[s, pl.ds(e * WIN, WIN), :] = jnp.where(pos[e:e + 1, :] == row, 1.0, 0.0).astype(BF16)
        return 0

    lax.fori_loop(0, 16, build, 0)
    t3(0)

    def clear(i, _):
        e, part = i // (ff // 256), i % (ff // 256)
        acc[e, :, pl.ds(pl.multiple_of(part * 512, 512), 512)] = jnp.zeros((rows, 512), F32)
        return 0

    lax.fori_loop(0, experts * 2 * ff // 512, clear, 0)
    _wait(xbuf.at[pl.ds(chunks * tokens, ff // 512 * tokens)], lsem)
    t4(0)
    t1(1)
    t0(2, 0, 1)

    def spread():
        held = [None] * experts
        over = [None] * experts
        done = [0] * experts
        for s in range(16):
            d = _dot(onehot[s], xbuf[pl.ds(s * tokens, tokens), :])
            size = 8 * ((s + 1) * slots // 8 - s * slots // 8)
            for e in range(experts):
                w = d[WIN * e:WIN * (e + 1)]
                v = [w[:size]] if over[e] is None else [w[:8] + over[e], w[8:size]]
                over[e] = w[size:size + 8] if (s + 1) * slots % 8 else None
                if held[e] is not None:
                    v = [held[e], *v]
                v = jnp.concatenate(v, 0) if len(v) > 1 else v[0]
                k = v.shape[0] // 16 * 16
                z[e, pl.ds(done[e], k), :] = v[:k].astype(BF16)
                held[e] = v[k:] if k < v.shape[0] else None
                done[e] += k

    def chunk(n, last):
        _wait(xbuf, xsem)
        spread()
        for e in range(experts):
            side = (chunks + experts * n + e) % 2
            if e + 1 < experts:
                weights(n, e + 1, 1 - side)
            elif not last:
                weights(n + 1, 0, 1 - side)
            if last:
                have(side, 0)
                have(side, 1)
                half_rows = rows // 32 * 16 + 16

                def finish(j, _):
                    at = pl.ds(pl.multiple_of(512 * j, 512), 512)
                    at_u = pl.ds(pl.multiple_of(ff + 512 * j, 512), 512)
                    there = pl.ds(pl.multiple_of(j * rows, 16), rows)
                    if e > 0:
                        _wait(xbuf.at[there], hsem.at[j])
                    for lo, size in ((0, half_rows), (half_rows, rows - half_rows)):
                        r = pl.ds(lo, size)
                        g = acc[e, r, at] + _dot(z[e, r, :], wbuf[side, 0, :, at])
                        u = acc[e, r, at_u] + _dot(z[e, r, :], wbuf[side, 1, :, at])
                        v = (g * jax.nn.sigmoid(g) * u).astype(BF16)
                        xbuf[pl.ds(pl.multiple_of(j * rows + lo, 16), size), :] = v
                    pltpu.make_async_copy(xbuf.at[there], h.at[e, :, at], hsem.at[j]).start()
                    return 0

                lax.fori_loop(0, ff // 512, finish, 0)
            else:
                for half in range(2):
                    have(side, half)
                    at = pl.ds(half * ff, ff)
                    acc[e, :, at] += _dot(z[e], wbuf[side, half])
                    point = 2 * e + half
                    if point == 0:
                        t2(n + 1)

                        @pl.when(n + 2 < chunks)
                        def _():
                            t0(n + 2, 2)
                    if point == 2:
                        @pl.when(n + 2 < chunks)
                        def _():
                            t1(n + 2)

                        @pl.when(n + 3 < chunks)
                        def _():
                            t0(n + 3, 0, 1)
                    if point == 3:
                        t3(n + 1)
                    if point == 4:
                        t4(n + 1)

    def most(n, _):
        chunk(n, False)
        return 0

    lax.fori_loop(0, chunks - 1, most, 0)
    chunk(chunks - 1, True)
    for k in range(ff // 512):
        _wait(xbuf.at[pl.ds(k * rows, rows)], hsem.at[k])
    meta_out.wait()
    _wait(mv.at[pl.ds(0, 15)], meta_send)
    _wait(xg.at[pl.ds(0, 15)], send_sem)


def _down_kernel(
    axis, chunks, experts, slots,
    h, hs, metag, wd, sd,
    y,
    hv, hsv, out32, wbuf, weight_t, mv, own, give, take, s1, s2, s3, r1, r2, r3, ost,
    hsem, lsem, wsem, give_sem, take_sem, credit, ss1, ss2, ss3, rs1, rs2, rs3, osem,
):
    me, bits, flip = _place(axis)
    tokens, rows = hs.shape[0], 16 * slots

    def cols(n):
        return pl.ds(pl.multiple_of(n * CB, CB), CB)

    def remote(src, dst, send, recv, mask):
        pltpu.make_async_remote_copy(
            src_ref=src, dst_ref=dst, send_sem=send, recv_sem=recv,
            device_id={axis: flip(mask)}, device_id_type=pl.DeviceIdType.MESH,
        ).start()

    def weights(n, e, side):
        src = wd.at[e, :, cols(n)] if e < experts else sd.at[:, cols(n)]
        pltpu.make_async_copy(src, wbuf.at[side], wsem.at[side]).start()

    copy = pltpu.make_async_copy(metag, mv, lsem)
    copy.start()
    pltpu.make_async_copy(h.at[0], hv.at[0], hsem.at[0]).start()
    weights(0, 0, 0)
    for e in range(1, experts):
        pltpu.make_async_copy(h.at[e], hv.at[e], hsem.at[e]).start()
    pltpu.make_async_copy(hs, hsv, hsem.at[experts]).start()
    _greet(axis, [flip(m) for m in (8, 4, 2, 1)])
    copy.wait()

    row = lax.broadcasted_iota(jnp.int32, (WIN, tokens), 0).astype(F32)
    rest = jnp.zeros((256 - experts * WIN, tokens), F32)

    def build(s, _):
        v = mv[s].astype(F32)
        shift = ((s * slots) % 8).astype(F32)
        hits = [
            jnp.where(v[e:e + 1, :] + shift == row, v[experts + e:experts + e + 1, :], 0.0) for e in range(experts)
        ]
        weight_t[s] = jnp.transpose(jnp.concatenate([*hits, rest], 0)).astype(BF16)
        return 0

    lax.fori_loop(0, 16, build, 0)
    for e in range(experts):
        out32[e, pl.ds(rows, 8), :] = jnp.zeros((8, CB), F32)

    def part(i):
        lo, size, dims = PARTS[i]
        return pl.ds(lo, size), dims

    def f32(ref, *at):
        return ref[at].astype(F32)

    def sum_at(n, block, r):
        p = n % LAG
        return own[p, block // 2, r, :] + f32(take, p, block // 2, r, slice(None))

    def free(n, ref, sem):
        @pl.when(n >= 2)
        def _():
            _wait(ref.at[n % 2], sem.at[n % 2])

    def stage1(n):
        p = n % 2
        _wait(take.at[n % LAG], take_sem.at[n % LAG])
        free(n, s1, ss1)
        for i in range(3):
            r, (a, b, c) = part(i)
            for k, q in enumerate((b + c, b, c, 0)):
                s1[p, k, r, :] = sum_at(n, q + a, r).astype(BF16)
                remote(s1.at[p, k, r], r1.at[n, k, r], ss1.at[p], rs1.at[n, i, k], a)

    def stage2(n):
        p = n % 2
        free(n, s2, ss2)
        for i in range(3):
            r, (a, b, c) = part(i)
            for k, q in enumerate((b + c, b)):
                _wait(r1.at[n, k, r], rs1.at[n, i, k])
                v = sum_at(n, q, r) + f32(r1, n, k, r, slice(None))
                s2[p, k, r, :] = v.astype(BF16)
                remote(s2.at[p, k, r], r2.at[n, k, r], ss2.at[p], rs2.at[n, i, k], b)

    def stage3(n):
        p = n % 2
        free(n, s3, ss3)
        for i in range(3):
            r, (a, b, c) = part(i)
            _wait(r1.at[n, 2, r], rs1.at[n, i, 2])
            _wait(r2.at[n, 0, r], rs2.at[n, i, 0])
            v = sum_at(n, c, r) + f32(r1, n, 2, r, slice(None)) + f32(r2, n, 0, r, slice(None))
            s3[p, r, :] = v.astype(BF16)
            remote(s3.at[p, r], r3.at[n, r], ss3.at[p], rs3.at[n, i], c)

    def stage4(n):
        p = n % 2
        free(n, ost, osem)
        for i in range(3):
            r, (a, b, c) = part(i)
            _wait(r1.at[n, 3, r], rs1.at[n, i, 3])
            _wait(r2.at[n, 1, r], rs2.at[n, i, 1])
            _wait(r3.at[n, r], rs3.at[n, i])
            v = sum_at(n, 0, r) + f32(r1, n, 3, r, slice(None)) + f32(r2, n, 1, r, slice(None))
            ost[p, r, :] = (v + f32(r3, n, r, slice(None))).astype(BF16)
        pltpu.make_async_copy(ost.at[p], y.at[:, cols(n)], osem.at[p]).start()
        pl.semaphore_signal(credit, inc=1, device_id={axis: flip(1)}, device_id_type=pl.DeviceIdType.MESH)

    def combine(r, core):
        s = flip(2 * r) - bits[1] + core
        at = pl.ds(pl.multiple_of(8 * ((s * slots) // 8), 8), WIN)
        rest = jnp.zeros((256 - experts * WIN, CB), F32)
        v = jnp.concatenate([*(out32[e, at, :] for e in range(experts)), rest], 0).astype(BF16)
        return _dot(weight_t[s], v)

    def late(n, k, stage):
        @pl.when((n >= k) & (n < chunks + k))
        def _():
            stage(n - k)

    def down(n, e):
        side = e % 2
        weights(n, e + 1, 1 - side)

        @pl.when(n == 0)
        def _():
            _wait(hv.at[e], hsem.at[e])

        _wait(wbuf.at[side], wsem.at[side])
        out32[e, pl.ds(0, rows), :] = _dot(hv[e], wbuf[side])

    def chunk(n, _):
        for e in range(experts):
            @pl.when(n < chunks)
            def _():
                down(n, e)

            if e == 0:
                late(n, 3, stage3)
                late(n, 1, stage1)
            if e == 1:
                late(n, 2, stage2)
            if e == 2:
                late(n, 3, stage4)

        @pl.when(n < chunks)
        def _():
            join(n)

        return 0

    def join(n):
        p = n % LAG

        @pl.when(n + 1 < chunks)
        def _():
            weights(n + 1, 0, 0)

        @pl.when(n >= 2)
        def _():
            _wait(give.at[n % 2], give_sem.at[n % 2])

        for r in range(8):
            give[n % 2, r] = combine(r, 1 - bits[1]).astype(BF16)

        @pl.when(n >= LAG)
        def _():
            pl.semaphore_wait(credit, 1)

        remote(give.at[n % 2], take.at[p], give_sem.at[n % 2], take_sem.at[p], 1)

        @pl.when(n == 0)
        def _():
            _wait(hsv, hsem.at[experts])

        _wait(wbuf.at[1], wsem.at[1])
        own[p, 0] = combine(0, bits[1]) + _dot(hsv[...], wbuf[1])
        for r in range(1, 8):
            own[p, r] = combine(r, bits[1])

    lax.fori_loop(0, chunks + LAG, chunk, 0)
    for p in range(2):
        _wait(give.at[p], give_sem.at[p])
        _wait(s1.at[p], ss1.at[p])
        _wait(s2.at[p], ss2.at[p])
        _wait(s3.at[p], ss3.at[p])
        _wait(ost.at[p], osem.at[p])
    pl.semaphore_wait(credit, LAG)


def solution(mesh):
    axis, members = "ep", mesh.shape["ep"]

    def local(x, expert, slot, gate, w_gate, w_up, w_down, s_gate, s_up, s_down):
        x, expert, slot, gate = x[0, 0], expert[0, 0], slot[0, 0], gate[0, 0]
        tokens, d = x.shape
        expert, slot, gate = expert.T, slot.T, gate.T
        experts, _, ff = w_gate.shape
        slots = 5 * tokens * expert.shape[0] // (4 * experts * members)
        rows = members * slots
        hbm, dma, vmem = pl.BlockSpec(memory_space=pl.ANY), pltpu.SemaphoreType.DMA, pltpu.VMEM
        table, chunks = (members, 16, tokens), d // CW
        _, metag, h, hs = pl.pallas_call(
            functools.partial(_up_kernel, axis, chunks, experts, slots),
            name="gather_up",
            out_shape=(
                jax.ShapeDtypeStruct((members, tokens, d), BF16),
                jax.ShapeDtypeStruct(table, BF16),
                jax.ShapeDtypeStruct((experts, rows, ff), BF16),
                jax.ShapeDtypeStruct((tokens, ff), BF16),
            ),
            in_specs=[hbm] * 8,
            out_specs=(hbm,) * 4,
            scratch_shapes=[
                vmem((members * tokens, CW), BF16),
                vmem((experts, rows, CW), BF16),
                vmem((experts, rows, 2 * ff), F32),
                vmem((2, 2, CW, ff), BF16),
                vmem((members, experts * WIN, tokens), BF16),
                vmem(expert.shape, jnp.int32),
                vmem(slot.shape, jnp.int32),
                vmem(gate.shape, F32),
                vmem(table, BF16),
                vmem(table, BF16),
                dma, dma((chunks, 3, 3)), dma((chunks,)), dma, dma, dma((2, 2)), dma, dma, dma((3,)), dma((ff // 512,)),
            ],
            compiler_params=pltpu.CompilerParams(
                collective_id=0, has_side_effects=True, vmem_limit_bytes=VMEM_LIMIT
            ),
        )(x, expert, slot, gate, w_gate, w_up, s_gate, s_up)
        chunks = d // CB
        y = pl.pallas_call(
            functools.partial(_down_kernel, axis, chunks, experts, slots),
            name="down_scatter",
            out_shape=jax.ShapeDtypeStruct((tokens, d), BF16),
            in_specs=[hbm] * 5,
            out_specs=hbm,
            scratch_shapes=[
                vmem((experts, rows, ff), BF16),
                vmem((tokens, ff), BF16),
                vmem((experts, rows + 8, CB), F32),
                vmem((2, ff, CB), BF16),
                vmem((members, tokens, 256), BF16),
                vmem(table, BF16),
                vmem((LAG, 8, tokens, CB), F32),
                vmem((2, 8, tokens, CB), BF16),
                vmem((LAG, 8, tokens, CB), BF16),
                vmem((2, 4, tokens, CB), BF16),
                vmem((2, 2, tokens, CB), BF16),
                vmem((2, tokens, CB), BF16),
                vmem((chunks, 4, tokens, CB), BF16),
                vmem((chunks, 2, tokens, CB), BF16),
                vmem((chunks, tokens, CB), BF16),
                vmem((2, tokens, CB), BF16),
                dma((experts + 1,)), dma, dma((2,)), dma((2,)), dma((LAG,)), pltpu.SemaphoreType.REGULAR,
                dma((2,)), dma((2,)), dma((2,)),
                dma((chunks, 3, 4)), dma((chunks, 3, 2)), dma((chunks, 3)), dma((2,)),
            ],
            compiler_params=pltpu.CompilerParams(
                collective_id=1, has_side_effects=True, vmem_limit_bytes=VMEM_LIMIT
            ),
        )(h, hs, metag, w_down, s_down)
        return y[None, None]

    tok = P("dp", "ep", None, None)
    own = P("ep", None, None)
    return jax.shard_map(
        local,
        mesh=mesh,
        in_specs=(tok, tok, tok, tok, own, own, own, P(), P(), P()),
        out_specs=tok,
        check_vma=False,
    )
```

time: 342 us -> 253 us (0.74)
  Pallas kernels: 334 us -> 250 us
  other arithmetic: 4.57 us -> 0 us
    pallas_call x2, Pallas kernels: 334 us -> 250 us  [the longest x1 132 us: local(): pl.pallas_call(functools.partial(_up_kernel, axis, chunks, experts, slots...]
where the time goes in v2:
time: 253 us
  Pallas kernels  250 us (99%)
  local copies, waits for them, and re-layouts  2.85 us (1%)
    pallas_call x1, Pallas kernels, local(): pl.pallas_call(functools.partial(_up_kernel, axis, chunks, experts, slots...  132 us
    pallas_call x1, Pallas kernels, local(): pl.pallas_call(functools.partial(_down_kernel, axis, chunks, experts, slo...  118 us

profile of v2, /device:TPU:0, one launch (start us, length us, event | category | flops | bytes accessed | tf_op | source)
XLA Modules:
  0.0 253.1 jit_solution(2247320143190947804)
XLA Ops:
  0.0 131.9 %gather_up.1 = (bf16[16,256,3584]{2,1,0:T(8,128)(2,1)}, bf16[16,16,256]{2,1,0:T(8,128)(2,1)}, bf16[3,848,2048]{2,1,0:T(8,128)(2,1)}, bf16[256,2048]{1,0:T(8,128)(2,1)}) custom-call(bf16[256,3584]{1,0:T(8,128)(2,1)} %bitcast.12, s32[8,256]{1,0:T(8,128)} %bitcast.13, s32[8,256]{1,0:T(8,128)} %bitcast.14, f32[8,256]{1,0:T(8,128)} %bitcast.15, ...), custom_call_target="tpu_custom_call" | custom-call | tf_op jit(solution)/shard_map/gather_up/pallas_call | solution.py:502
  131.9 118.4 %down_scatter.1 = bf16[256,3584]{1,0:T(8,128)(2,1)} custom-call(bf16[3,848,2048]{2,1,0:T(8,128)(2,1)} %get-tuple-element.8.h, bf16[256,2048]{1,0:T(8,128)(2,1)} %get-tuple-element.9.hs, bf16[16,16,256]{2,1,0:T(8,128)(2,1)} %get-tuple-element.10.metag, bf16[3,2048,3584]{2,1,0:T(8,128)(2,1)} %wd.1, bf16[2048,3584]{1,0:T(8,128)(2,1)} %sd.1), custom_call_target="tpu_custom_call" | custom-call | tf_op jit(solution)/shard_map/down_scatter/pallas_call | solution.py:531
  250.3 2.8 %copy.12 = bf16[1,1,256,3584]{3,2,1,0:T(8,128)(2,1)} copy(bf16[1,1,256,3584]{3,2,1,0:T(8,128)(2,1)} %bitcast.11) | data formatting | bytes 3670016

commit v3 on v2

--- a/solution.py
+++ b/solution.py
@@ -195,14 +195,13 @@
         return 0
 
     lax.fori_loop(0, 16, build, 0)
-    t3(0)
-
     def clear(i, _):
         e, part = i // (ff // 256), i % (ff // 256)
         acc[e, :, pl.ds(pl.multiple_of(part * 512, 512), 512)] = jnp.zeros((rows, 512), F32)
         return 0
 
     lax.fori_loop(0, experts * 2 * ff // 512, clear, 0)
+    t3(0)
     _wait(xbuf.at[pl.ds(chunks * tokens, ff // 512 * tokens)], lsem)
     t4(0)
     t1(1)
@@ -229,6 +228,12 @@
 
     def chunk(n, last):
         _wait(xbuf, xsem)
+        if not last:
+            t2(n + 1)
+
+            @pl.when(n + 2 < chunks)
+            def _():
+                t0(n + 2, 2)
         spread()
         for e in range(experts):
             side = (chunks + experts * n + e) % 2
@@ -263,12 +268,6 @@
                     at = pl.ds(half * ff, ff)
                     acc[e, :, at] += _dot(z[e], wbuf[side, half])
                     point = 2 * e + half
-                    if point == 0:
-                        t2(n + 1)
-
-                        @pl.when(n + 2 < chunks)
-                        def _():
-                            t0(n + 2, 2)
                     if point == 2:
                         @pl.when(n + 2 < chunks)
                         def _():
@@ -459,14 +458,15 @@
         def _():
             _wait(give.at[n % 2], give_sem.at[n % 2])
 
-        for r in range(8):
-            give[n % 2, r] = combine(r, 1 - bits[1]).astype(BF16)
-
         @pl.when(n >= LAG)
         def _():
             pl.semaphore_wait(credit, 1)
 
-        remote(give.at[n % 2], take.at[p], give_sem.at[n % 2], take_sem.at[p], 1)
+        for lo in (0, 4):
+            for r in range(lo, lo + 4):
+                give[n % 2, r] = combine(r, 1 - bits[1]).astype(BF16)
+            some = pl.ds(lo, 4)
+            remote(give.at[n % 2, some], take.at[p, some], give_sem.at[n % 2], take_sem.at[p], 1)
 
         @pl.when(n == 0)
         def _():

time: 253 us -> 252 us (level)
  no operation moved by 1% of the time
where the time goes in v3:
time: 252 us
  Pallas kernels  249 us (99%)
  local copies, waits for them, and re-layouts  2.85 us (1%)
    pallas_call x1, Pallas kernels, local(): pl.pallas_call(functools.partial(_up_kernel, axis, chunks, experts, slots...  132 us
    pallas_call x1, Pallas kernels, local(): pl.pallas_call(functools.partial(_down_kernel, axis, chunks, experts, slo...  118 us

profile of v3, /device:TPU:0, one launch (start us, length us, event | category | flops | bytes accessed | tf_op | source)
XLA Modules:
  0.0 252.0 jit_solution(15366778237231873851)
XLA Ops:
  0.0 131.6 %gather_up.1 = (bf16[16,256,3584]{2,1,0:T(8,128)(2,1)}, bf16[16,16,256]{2,1,0:T(8,128)(2,1)}, bf16[3,848,2048]{2,1,0:T(8,128)(2,1)}, bf16[256,2048]{1,0:T(8,128)(2,1)}) custom-call(bf16[256,3584]{1,0:T(8,128)(2,1)} %bitcast.12, s32[8,256]{1,0:T(8,128)} %bitcast.13, s32[8,256]{1,0:T(8,128)} %bitcast.14, f32[8,256]{1,0:T(8,128)} %bitcast.15, ...), custom_call_target="tpu_custom_call" | custom-call | tf_op jit(solution)/shard_map/gather_up/pallas_call | solution.py:502
  131.6 117.5 %down_scatter.1 = bf16[256,3584]{1,0:T(8,128)(2,1)} custom-call(bf16[3,848,2048]{2,1,0:T(8,128)(2,1)} %get-tuple-element.8.h, bf16[256,2048]{1,0:T(8,128)(2,1)} %get-tuple-element.9.hs, bf16[16,16,256]{2,1,0:T(8,128)(2,1)} %get-tuple-element.10.metag, bf16[3,2048,3584]{2,1,0:T(8,128)(2,1)} %wd.1, bf16[2048,3584]{1,0:T(8,128)(2,1)} %sd.1), custom_call_target="tpu_custom_call" | custom-call | tf_op jit(solution)/shard_map/down_scatter/pallas_call | solution.py:531
  249.1 2.8 %copy.12 = bf16[1,1,256,3584]{3,2,1,0:T(8,128)(2,1)} copy(bf16[1,1,256,3584]{3,2,1,0:T(8,128)(2,1)} %bitcast.11) | data formatting | bytes 3670016
